TPU v7x, 32 devices: a whole 2x2x4 slice. The times are simulated.
32 devices in a mesh: outer: 4 (over y, x), dev: 8 (over z, core).
Axes of the slice: x: 2, y: 2, z: 4, core: 2. Of those that a mesh axis runs over, the one named last changes fastest.
Arguments:
- documents: bfloat16 [6144, 4096], P(('outer', 'dev')), may hold values from -8 to 8
- cluster_of: int32 [6144], replicated, may hold values from 0 to 31, as said below
- neighbours: int32 [32, 4], replicated, may hold values from 0 to 31, as said below
- sharpness: float32 [32], replicated, may hold values from 32 to 64
Outputs:
- density: float32 [6144], P(('outer', 'dev'))
Inputs may be any that keep to these rules, and one draw needn't show every extreme that they name: `cluster_of`: rows b * 192 to (b + 1) * 192 - 1 form block b. Block b names only clusters g * 8 to (g + 1) * 8 - 1, with g = b // 8, and names no cluster more than 48 times; in each group g some cluster is named exactly 48 times by every block of that group; every cluster is named by some row. `neighbours`: row c, with c = g * 8 + h, lists in order the clusters g * 8 + ((h - 1) mod 8), g * 8 + ((h + 1) mod 8), ((g - 1) mod 4) * 8 + ((h + b) mod 8) and ((g + 1) mod 4) * 8 + ((h + d) mod 8), with b and d each in -1, 0, 1.
All inputs are finite; a program needn't handle non-finite values.
Results may differ from a plain program's by a relative error of at most 0.00047.
Values may be sent and summed in bfloat16 or wider, within the bound.
A program may use at most 128 MiB of HBM per device.

v0:
```python
import math
import jax
import jax.numpy as jnp
from jax import lax
from jax.sharding import PartitionSpec as P


def passed_along(block, axis, distance):
    devices = range(lax.axis_size(axis))
    route = [((i - distance) % len(devices), i) for i in devices]
    return lax.ppermute(block, axis, route)


def kernel_block(queries, others, pair_gain):
    products = jnp.einsum("qe,ke->qk", queries, others, preferred_element_type=jnp.float32)
    return jnp.exp(pair_gain * products)


def shards(documents, cluster_of, neighbours, sharpness):
    groups = lax.axis_size("outer")
    owners = lax.axis_size("dev")
    tokens_here = documents.shape[0]
    feature_width = documents.shape[1]
    capacity = max(2, 2 * tokens_here // owners)
    slot_count = owners * capacity
    group_index = lax.axis_index("outer")
    owner_index = lax.axis_index("dev")
    own_cluster = group_index * owners + owner_index
    block_labels = cluster_of.reshape(groups * owners, tokens_here)
    group_of_block = jnp.arange(groups * owners, dtype=jnp.int32) // owners
    local_labels = block_labels - group_of_block[:, None] * owners
    owner_range = jnp.arange(owners, dtype=jnp.int32)
    per_block = jnp.sum(
        (local_labels[:, :, None] == owner_range).astype(jnp.int32), axis=1
    ).reshape(groups, owners, owners)
    cluster_sizes = jnp.sum(per_block, axis=1).reshape(-1)
    own_labels = lax.dynamic_index_in_dim(local_labels, own_cluster, 0, keepdims=False)
    ordinal = jnp.arange(tokens_here, dtype=jnp.int32)
    earlier = ordinal[None, :] < ordinal[:, None]
    repeats = jnp.sum(
        ((own_labels[:, None] == own_labels[None, :]) & earlier).astype(jnp.int32), axis=1
    )
    target = own_labels * capacity + repeats
    placing = (jnp.arange(slot_count, dtype=jnp.int32)[:, None] == target[None, :]).astype(
        jnp.bfloat16
    )
    outgoing = jnp.dot(placing, documents, preferred_element_type=jnp.float32).astype(jnp.bfloat16)
    arrived = lax.all_to_all(
        outgoing.reshape(owners, capacity, feature_width),
        "dev",
        split_axis=0,
        concat_axis=0,
        tiled=True,
    ).reshape(slot_count, feature_width)

    def slot_mask(group_at, owner_at):
        senders = per_block[group_at, :, owner_at]
        return (
            (jnp.arange(capacity, dtype=jnp.int32)[None, :] < senders[:, None])
            .astype(jnp.float32)
            .reshape(-1)
        )

    present = slot_mask(group_index, owner_index)
    centre = jnp.dot(
        present.astype(jnp.bfloat16)[None, :], arrived, preferred_element_type=jnp.float32
    )[0]
    centre = centre / cluster_sizes[own_cluster].astype(jnp.float32)
    centred = arrived.astype(jnp.float32) - centre[None, :]
    scaling = lax.rsqrt(jnp.mean(centred * centred, axis=1) + 1e-06) / math.sqrt(feature_width)
    unit_rows = (centred * (scaling * present)[:, None]).astype(jnp.bfloat16)
    own_gain = sharpness[own_cluster]
    listed = neighbours[own_cluster]
    off_diagonal = 1.0 - jnp.eye(slot_count, dtype=jnp.float32)
    running = jnp.sum(
        kernel_block(unit_rows, unit_rows, own_gain) * (present[None, :] * off_diagonal), axis=1
    )
    beside = [passed_along(unit_rows, "dev", offset) for offset in (1, -1)]
    vertical = []
    for direction, position in ((1, 2), (-1, 3)):
        receiver_group = (group_index + direction) % groups
        wanted = neighbours[receiver_group * owners + owner_index, position]
        delta = (wanted % owners - owner_index + owners) % owners
        picked_rows = jnp.where(
            delta == 1, beside[1], jnp.where(delta == owners - 1, beside[0], unit_rows)
        )
        vertical.append(passed_along(picked_rows, "outer", direction))
    key_sets = [beside[0], beside[1], vertical[0], vertical[1]]
    for position in range(4):
        partner = listed[position]
        partner_group_at = partner // owners
        partner_owner_at = partner % owners
        partner_partner = partner_group_at * owners + partner_owner_at
        pair_gain = 0.5 * (own_gain + sharpness[partner_partner])
        partner = partner_partner
        kernel_terms = kernel_block(unit_rows, key_sets[position], pair_gain)
        key_mask = slot_mask(partner_group_at, partner_owner_at)
        running = running + jnp.sum(kernel_terms * key_mask[None, :], axis=1)
    partner_count = cluster_sizes[own_cluster] - 1 + jnp.sum(cluster_sizes[listed])
    slot_density = jnp.log(running / partner_count.astype(jnp.float32))
    answered = lax.all_to_all(
        slot_density.reshape(owners, capacity), "dev", split_axis=0, concat_axis=0, tiled=True
    ).reshape(-1)
    return answered[target]


def lookup(table, index):
    hit = index[:, None] == jnp.arange(table.shape[0], dtype=jnp.int32)[None, :]
    return jnp.sum(jnp.where(hit, table[None, :], jnp.zeros((), table.dtype)), axis=1)


def gathered(documents, cluster_of, neighbours, sharpness):
    groups = lax.axis_size("outer")
    owners = lax.axis_size("dev")
    tokens_here, feature_width = documents.shape
    group_index = lax.axis_index("outer")
    owner_index = lax.axis_index("dev")
    clusters = groups * owners
    group_rows = owners * tokens_here
    cluster_range = jnp.arange(clusters, dtype=jnp.int32)
    sizes = jnp.sum((cluster_of[:, None] == cluster_range[None, :]).astype(jnp.int32), axis=0)

    def labels_at(group_at):
        start = (group_at * owners + owner_index) * tokens_here
        return lax.dynamic_slice_in_dim(cluster_of, start, tokens_here)

    previous = (group_index + groups - 1) % groups
    following = (group_index + 1) % groups
    own = labels_at(group_index)
    local = own - group_index * owners
    local_range = jnp.arange(owners, dtype=jnp.int32)
    member = (local_range[:, None] == local[None, :]).astype(jnp.bfloat16)
    sums = lax.psum(jnp.dot(member, documents, preferred_element_type=jnp.float32), "dev")
    own_sizes = lax.dynamic_slice_in_dim(sizes, group_index * owners, owners)
    means = sums / own_sizes.astype(jnp.float32)[:, None]
    centre = jnp.dot(
        member.astype(jnp.float32).T,
        means,
        precision=lax.Precision.HIGHEST,
        preferred_element_type=jnp.float32,
    )
    centred = documents.astype(jnp.float32) - centre
    scaling = lax.rsqrt(jnp.mean(centred * centred, axis=1) + 1e-06) / math.sqrt(feature_width)
    unit_rows = (centred * scaling[:, None]).astype(jnp.bfloat16)
    from_previous = passed_along(unit_rows, "outer", 1)
    from_following = passed_along(unit_rows, "outer", -1)
    keys = lax.all_gather(unit_rows, "dev", axis=0, tiled=True)
    key_labels = lax.dynamic_slice_in_dim(cluster_of, group_index * group_rows, group_rows)
    key_gain = lookup(sharpness, key_labels)

    def partial(queries, labels, positions, own_too):
        products = jnp.einsum("qe,ke->qk", queries, keys, preferred_element_type=jnp.float32)
        gain = 0.5 * (lookup(sharpness, labels)[:, None] + key_gain[None, :])
        wanted = jnp.zeros(products.shape, jnp.bool_)
        for position in positions:
            listed = lookup(neighbours[:, position], labels)
            wanted = wanted | (listed[:, None] == key_labels[None, :])
        if own_too:
            at = owner_index * tokens_here + jnp.arange(tokens_here, dtype=jnp.int32)
            other = at[:, None] != jnp.arange(group_rows, dtype=jnp.int32)[None, :]
            wanted = wanted | (labels[:, None] == key_labels[None, :]) & other
        return jnp.sum(jnp.where(wanted, jnp.exp(gain * products), 0.0), axis=1)

    back_previous = partial(from_previous, labels_at(previous), (3,), False)
    back_following = partial(from_following, labels_at(following), (2,), False)
    running = partial(unit_rows, own, (0, 1), True)
    running = running + passed_along(back_previous, "outer", -1)
    running = running + passed_along(back_following, "outer", 1)
    counts = sizes - 1
    for position in range(neighbours.shape[1]):
        counts = counts + lookup(sizes, neighbours[:, position])
    return jnp.log(running / lookup(counts, own).astype(jnp.float32))


def solution(mesh):
    small = mesh.shape["dev"] <= 8
    in_specs = (P(("outer", "dev"), None), P(), P(), P())
    out_specs = P(("outer", "dev"))
    body = gathered if small else shards
    return jax.shard_map(body, mesh=mesh, in_specs=in_specs, out_specs=out_specs, check_vma=False)
```

profile of v0, /device:TPU:0, one launch (start us, length us, event | category | flops | bytes accessed | tf_op | source)
XLA Modules:
  0.0 226.7 jit_solution(15810836763792392852)
XLA Ops:
  6.5 0.0 all-reduce.2.cloned.1.call-start
  6.5 0.9 broadcast_subtract_fusion
  7.5 2.4 %fusion.13 = f32[8,4096]{1,0:T(8,128)} fusion(bf16[192,4096]{1,0:T(8,128)(2,1)} %param.4, s32[192]{0:T(256)S(1)} %get-tuple-element.15), kind=kOutput, calls=%fused_computation.44 | convolution fusion | flops 12584448 | bytes 1704704 | tf_op jit(solution)/shard_map/dot_general | solution.py:133
  9.8 0.0 all-reduce.2.cloned.1.call-update
  9.9 0.0 all-gather.2.cloned.1.call-start
  9.9 0.2 convert_reduce_fusion
  10.1 0.1 dynamic-slice_convert_fusion
  10.2 57.5 %all-reduce.2.cloned.1.call-done = f32[8,4096]{1,0:T(8,128)} async-done(((f32[8,4096]{1,0:T(8,128)}), f32[8,4096]{1,0:T(8,128)}) %all-reduce.2.cloned.1.call-update) | async-done | bytes 131088 | tf_op jit(solution)/shard_map/psum | solution.py:133
  67.7 2.8 %multiply_reduce_fusion = (f32[192]{0:T(256)S(1)}, f32[192,4096]{1,0:T(8,128)S(1)}) fusion(f32[8,4096]{1,0:T(8,128)} %all-reduce.2.cloned.1.call-done, f32[8]{0:T(128)S(1)} %dynamic-slice_convert_fusion, s32[192]{0:T(256)S(1)} %get-tuple-element.15, bf16[192,4096]{1,0:T(8,128)(2,1)S(1)} %copy-done.1), kind=kOutput, calls=%fused_computation.2 | convolution fusion | flops 78677312 | bytes 4851232 | tf_op jit(solution)/shard_map/dot_general | solution.py:136
  70.5 1.5 multiply_convert_fusion
  72.0 0.0 all-gather.2.cloned.1.call-update
  72.1 1.4 copy-done
  73.4 2.4 %collective-permute-start.2 = (bf16[192,4096]{1,0:T(8,128)(2,1)S(1)}, bf16[192,4096]{1,0:T(8,128)(2,1)S(1)}, u32[]{:S(2)}, u32[]{:S(2)}) collective-permute-start(bf16[192,4096]{1,0:T(8,128)(2,1)S(1)} %copy-done), channel_id=1, source_target_pairs={{8,0},{16,8},{24,16},{0,24},{9,1},{17,9},{25,17},{1,25},{10,2},{18... | collective-permute-start | bytes 4718600 | tf_op jit(solution)/shard_map/ppermute | solution.py:11
  75.8 0.1 dynamic_slice.16
  75.9 0.1 select_reduce_fusion.3
  76.0 0.1 select_reduce_fusion.5
  76.1 0.1 select_reduce_fusion.4
  76.2 0.1 collective-permute-start
  76.3 0.2 select_reduce_fusion.12
  76.5 0.1 select_reduce_fusion.8
  76.6 0.1 select_reduce_fusion
  76.7 34.0 %collective-permute-done.2 = bf16[192,4096]{1,0:T(8,128)(2,1)S(1)} collective-permute-done((bf16[192,4096]{1,0:T(8,128)(2,1)S(1)}, bf16[192,4096]{1,0:T(8,128)(2,1)S(1)}, u32[]{:S(2)}, u32[]{:S(2)}) %collective-permute-start.2) | collective-permute-done | bytes 1572896 | tf_op jit(solution)/shard_map/ppermute | solution.py:11
  110.7 77.3 %all-gather.2.cloned.1.call-done = bf16[1536,4096]{1,0:T(8,128)(2,1)} async-done(((bf16[192,4096]{1,0:T(8,128)(2,1)}), bf16[1536,4096]{1,0:T(8,128)(2,1)}) %all-gather.2.cloned.1.call-update) | async-done | bytes 12582928 | tf_op jit(solution)/shard_map/all_gather | solution.py:147
  188.0 9.1 %fusion.8 = f32[192]{0:T(256)S(1)} fusion(bf16[192,4096]{1,0:T(8,128)(2,1)S(1)} %collective-permute-done.2, bf16[1536,4096]{1,0:T(8,128)(2,1)} %all-gather.2.cloned.1.call-done, f32[192]{0:T(256)S(1)} %get-tuple-element.9, f32[1536]{0:T(1024)S(1)} %select_reduce_fusion, s32[1536]{0:T(1024)S(1)} %dynamic_slice.16, s32[192]{0:T(256)S(1)} %select_reduce_fusion.3), kind=kOutput, calls=%fused_computation.14 | convolution fusion | flops 2417688320 | bytes 14170368 | tf_op jit(solution)/shard_map/qe,ke->qk/dot_general | solution.py:152
  197.1 1.5 collective-permute-start.3
  198.6 0.0 collective-permute-done
  198.6 9.6 %fusion.7 = f32[192]{0:T(256)S(1)} fusion(bf16[192,4096]{1,0:T(8,128)(2,1)} %collective-permute-done, bf16[1536,4096]{1,0:T(8,128)(2,1)} %all-gather.2.cloned.1.call-done, f32[192]{0:T(256)S(1)} %get-tuple-element.8, f32[1536]{0:T(1024)S(1)} %select_reduce_fusion, s32[1536]{0:T(1024)S(1)} %dynamic_slice.16, s32[192]{0:T(256)S(1)} %select_reduce_fusion.5), kind=kOutput, calls=%fused_computation.13 | convolution fusion | flops 2417688320 | bytes 14170368 | tf_op jit(solution)/shard_map/qe,ke->qk/dot_general | solution.py:152
  208.2 1.7 collective-permute-start.1
  209.9 9.4 %fusion.6 = f32[192]{0:T(256)S(1)} fusion(bf16[192,4096]{1,0:T(8,128)(2,1)S(1)} %copy-done, bf16[1536,4096]{1,0:T(8,128)(2,1)} %all-gather.2.cloned.1.call-done, f32[1536]{0:T(1024)S(1)} %select_reduce_fusion, f32[192]{0:T(256)S(1)} %get-tuple-element.10, s32[192]{0:T(256)S(1)} %iota_add_fusion, s32[1536]{0:T(1024)S(1)} %dynamic_slice.16, ...), kind=kOutput, calls=%fused_computation.12 | convolution fusion | flops 2419457792 | bytes 14172672 | tf_op jit(solution)/shard_map/qe,ke->qk/dot_general | solution.py:152
  219.3 0.0 collective-permute-done.3
  219.3 0.0 collective-permute-done.1
  219.3 0.6 fusion.16
  (13 shorter events, 0.0 us)
Async XLA Ops:
  6.5 3.4 %copy-start.2 = (s32[6144]{0:T(1024)S(1)}, s32[6144]{0:T(1024)}, u32[]{:S(2)}) copy-start(s32[6144]{0:T(1024)} %param.5) | copy-start | bytes 73732
  6.5 61.2 %copy-start.1 = (bf16[192,4096]{1,0:T(8,128)(2,1)S(1)}, bf16[192,4096]{1,0:T(8,128)(2,1)}, u32[]{:S(2)}) copy-start(bf16[192,4096]{1,0:T(8,128)(2,1)} %param.4) | copy-start | bytes 4718596
  6.5 61.2 %all-reduce.2.cloned.1.call-start = ((), (), s32[]{:S(2)}) async-start(), calls=%async_computation | async-start | bytes 262144 | tf_op jit(solution)/shard_map/psum | solution.py:133
  9.9 178.2 %all-gather.2.cloned.1.call-start = ((), (), s32[]{:S(2)}) async-start(), calls=%async_computation.1 | async-start | bytes 14155776 | tf_op jit(solution)/shard_map/all_gather | solution.py:147
  72.0 1.4 copy-start
  72.0 3.9 %copy-start.3 = (s32[32,4]{0,1:T(4,128)S(1)}, s32[32,4]{0,1:T(4,128)}, u32[]{:S(2)}) copy-start(s32[32,4]{0,1:T(4,128)} %param.6) | copy-start | bytes 1540
  72.0 4.0 %copy-start.4 = (f32[32]{0:T(128)S(1)}, f32[32]{0:T(128)}, u32[]{:S(2)}) copy-start(f32[32]{0:T(128)} %param.7) | copy-start | bytes 388
  73.4 37.3 %collective-permute-start.2 = (bf16[192,4096]{1,0:T(8,128)(2,1)S(1)}, bf16[192,4096]{1,0:T(8,128)(2,1)S(1)}, u32[]{:S(2)}, u32[]{:S(2)}) collective-permute-start(bf16[192,4096]{1,0:T(8,128)(2,1)S(1)} %copy-done), channel_id=1, source_target_pairs={{8,0},{16,8},{24,16},{0,24},{9,1},{17,9},{25,17},{1,25},{10,2},{18... | collective-permute-start | bytes 4718600 | tf_op jit(solution)/shard_map/ppermute | solution.py:11
  76.2 122.4 %collective-permute-start = (bf16[192,4096]{1,0:T(8,128)(2,1)S(1)}, bf16[192,4096]{1,0:T(8,128)(2,1)}, u32[]{:S(2)}, u32[]{:S(2)}) collective-permute-start(bf16[192,4096]{1,0:T(8,128)(2,1)S(1)} %copy-done), channel_id=1, source_target_pairs={{24,0},{0,8},{8,16},{16,24},{25,1},{1,9},{9,17},{17,25},{26,2},{2,... | collective-permute-start | bytes 4718600 | tf_op jit(solution)/shard_map/ppermute | solution.py:11
  197.1 22.2 %collective-permute-start.3 = (f32[192]{0:T(256)S(1)}, f32[192]{0:T(256)S(1)}, u32[]{:S(2)}, u32[]{:S(2)}) collective-permute-start(f32[192]{0:T(256)S(1)} %fusion.8), channel_id=1, source_target_pairs={{24,0},{0,8},{8,16},{16,24},{25,1},{1,9},{9,17},{17,25},{26,2},{2,... | collective-permute-start | bytes 2312 | tf_op jit(solution)/shard_map/ppermute | solution.py:11
  208.2 11.1 %collective-permute-start.1 = (f32[192]{0:T(256)S(1)}, f32[192]{0:T(256)S(1)}, u32[]{:S(2)}, u32[]{:S(2)}) collective-permute-start(f32[192]{0:T(256)S(1)} %fusion.7), channel_id=1, source_target_pairs={{8,0},{16,8},{24,16},{0,24},{9,1},{17,9},{25,17},{1,25},{10,2},{18... | collective-permute-start | bytes 2312 | tf_op jit(solution)/shard_map/ppermute | solution.py:11
Sparse Core Ops, SparseCore 0:
  10.0 57.6 all-reduce.1
  72.2 115.8 all-gather.1
where the time goes:
time: 227 us
  waiting for transfers between devices  169 us (74%)
  matrix products  33.2 us (15%)
  between operations  13.5 us (6%)
  starting transfers between devices  5.69 us (3%)
  other arithmetic  4.04 us (2%)
    all_gather x1, waiting for transfers between devices, gathered(): keys = lax.all_gather(unit_rows, 'dev', axis=0, tiled=True)  77.3 us
    psum x1, waiting for transfers between devices, gathered(): lax.psum(jnp.dot(member, documents, preferred_element_type=jnp.float32),...  57.5 us
    ppermute x4, waiting for transfers between devices, passed_along(): return lax.ppermute(block, axis, route)  34 us
    dot_general x3, matrix products, partial(): jnp.einsum('qe,ke->qk', queries, keys, preferred_element_type=jnp.float32)  28 us
    ppermute x4, starting transfers between devices, passed_along(): return lax.ppermute(block, axis, route)  5.65 us
  transfers between devices with their start and end apart: 6, of which 3 were waited for; matrix products, arithmetic and copies ran while one was open for 13% of the time, Pallas kernels for 0%

commit v1 on v0

--- a/solution.py
+++ b/solution.py
@@ -130,7 +130,10 @@
     local = own - group_index * owners
     local_range = jnp.arange(owners, dtype=jnp.int32)
     member = (local_range[:, None] == local[None, :]).astype(jnp.bfloat16)
-    sums = lax.psum(jnp.dot(member, documents, preferred_element_type=jnp.float32), "dev")
+    sums = jnp.sum(
+        lax.all_gather(jnp.dot(member, documents, preferred_element_type=jnp.float32), "dev"),
+        axis=0,
+    )
     own_sizes = lax.dynamic_slice_in_dim(sizes, group_index * owners, owners)
     means = sums / own_sizes.astype(jnp.float32)[:, None]
     centre = jnp.dot(

time: 227 us -> 195 us (0.86)
  waiting for transfers between devices: 169 us -> 137 us
    psum x1 -> x0, waiting for transfers between devices: 57.5 us -> none  [gathered(): lax.psum(jnp.dot(member, documents, preferred_element_type=jnp.float32),...]
    all_gather x0 -> x1, waiting for transfers between devices: none -> 24.8 us  [gathered(): lax.all_gather(jnp.dot(member, documents, preferred_element_type=jnp.floa...]
  transfers between devices with their start and end apart: 6 -> 6, of which waited for: 3 -> 3; matrix products, arithmetic and copies ran while one was open for 13% -> 15% of each run, Pallas kernels for 0% -> 0%
where the time goes in v1:
time: 195 us
  waiting for transfers between devices  137 us (70%)
  matrix products  32.4 us (17%)
  between operations  13.5 us (7%)
  starting transfers between devices  5.7 us (3%)
  other arithmetic  5.27 us (3%)
    all_gather x1, waiting for transfers between devices, gathered(): keys = lax.all_gather(unit_rows, 'dev', axis=0, tiled=True)  77.8 us
    ppermute x4, waiting for transfers between devices, passed_along(): return lax.ppermute(block, axis, route)  34 us
    dot_general x3, matrix products, partial(): jnp.einsum('qe,ke->qk', queries, keys, preferred_element_type=jnp.float32)  28 us
    all_gather x1, waiting for transfers between devices, gathered(): lax.all_gather(jnp.dot(member, documents, preferred_element_type=jnp.floa...  24.8 us
    ppermute x4, starting transfers between devices, passed_along(): return lax.ppermute(block, axis, route)  5.65 us
  transfers between devices with their start and end apart: 6, of which 3 were waited for; matrix products, arithmetic and copies ran while one was open for 15% of the time, Pallas kernels for 0%

profile of v1, /device:TPU:0, one launch (start us, length us, event | category | flops | bytes accessed | tf_op | source)
XLA Modules:
  0.0 195.0 jit_solution(17361632254989044931)
XLA Ops:
  6.5 0.9 broadcast_subtract_fusion
  7.4 2.5 %fusion.13 = f32[8,4096]{1,0:T(8,128)} fusion(bf16[192,4096]{1,0:T(8,128)(2,1)} %param.4, s32[192]{0:T(256)S(1)} %get-tuple-element.15), kind=kOutput, calls=%fused_computation.45 | convolution fusion | flops 12584448 | bytes 1704704 | tf_op jit(solution)/shard_map/dot_general | solution.py:134
  9.9 0.0 all-gather.6.cloned.1.call-update
  9.9 0.0 all-gather.4.cloned.1.call-start
  10.0 0.2 convert_reduce_fusion
  10.2 0.1 dynamic-slice_convert_fusion
  10.3 24.8 %all-gather.6.cloned.1.call-done = f32[64,4096]{1,0:T(8,128)} async-done(((f32[8,4096]{1,0:T(8,128)}), f32[64,4096]{1,0:T(8,128)}) %all-gather.6.cloned.1.call-update) | async-done | bytes 1048592 | tf_op jit(solution)/shard_map/all_gather | solution.py:134
  35.1 1.3 bitcast_reduce_fusion
  36.4 1.9 multiply_reduce_fusion
  38.2 1.5 multiply_convert_fusion
  39.8 0.0 all-gather.4.cloned.1.call-update
  39.8 1.4 copy-done
  41.2 2.4 %collective-permute-start.2 = (bf16[192,4096]{1,0:T(8,128)(2,1)S(1)}, bf16[192,4096]{1,0:T(8,128)(2,1)S(1)}, u32[]{:S(2)}, u32[]{:S(2)}) collective-permute-start(bf16[192,4096]{1,0:T(8,128)(2,1)S(1)} %copy-done), channel_id=1, source_target_pairs={{8,0},{16,8},{24,16},{0,24},{9,1},{17,9},{25,17},{1,25},{10,2},{18... | collective-permute-start | bytes 4718600 | tf_op jit(solution)/shard_map/ppermute | solution.py:11
  43.6 0.1 dynamic_slice.16
  43.6 0.1 select_reduce_fusion.3
  43.7 0.1 select_reduce_fusion.5
  43.8 0.1 select_reduce_fusion.4
  43.9 0.1 collective-permute-start
  44.0 0.2 select_reduce_fusion.12
  44.3 0.1 select_reduce_fusion.8
  44.4 0.1 select_reduce_fusion
  44.5 34.0 %collective-permute-done.2 = bf16[192,4096]{1,0:T(8,128)(2,1)S(1)} collective-permute-done((bf16[192,4096]{1,0:T(8,128)(2,1)S(1)}, bf16[192,4096]{1,0:T(8,128)(2,1)S(1)}, u32[]{:S(2)}, u32[]{:S(2)}) %collective-permute-start.2) | collective-permute-done | bytes 1572896 | tf_op jit(solution)/shard_map/ppermute | solution.py:11
  78.4 77.8 %all-gather.4.cloned.1.call-done = bf16[1536,4096]{1,0:T(8,128)(2,1)} async-done(((bf16[192,4096]{1,0:T(8,128)(2,1)}), bf16[1536,4096]{1,0:T(8,128)(2,1)}) %all-gather.4.cloned.1.call-update) | async-done | bytes 12582928 | tf_op jit(solution)/shard_map/all_gather | solution.py:150
  156.3 9.1 %fusion.8 = f32[192]{0:T(256)S(1)} fusion(bf16[192,4096]{1,0:T(8,128)(2,1)S(1)} %collective-permute-done.2, bf16[1536,4096]{1,0:T(8,128)(2,1)} %all-gather.4.cloned.1.call-done, f32[192]{0:T(256)S(1)} %get-tuple-element.9, f32[1536]{0:T(1024)S(1)} %select_reduce_fusion, s32[1536]{0:T(1024)S(1)} %dynamic_slice.16, s32[192]{0:T(256)S(1)} %select_reduce_fusion.3), kind=kOutput, calls=%fused_computation.14 | convolution fusion | flops 2417688320 | bytes 14170368 | tf_op jit(solution)/shard_map/qe,ke->qk/dot_general | solution.py:155
  165.3 1.5 collective-permute-start.3
  166.9 0.0 collective-permute-done
  166.9 9.6 %fusion.7 = f32[192]{0:T(256)S(1)} fusion(bf16[192,4096]{1,0:T(8,128)(2,1)} %collective-permute-done, bf16[1536,4096]{1,0:T(8,128)(2,1)} %all-gather.4.cloned.1.call-done, f32[192]{0:T(256)S(1)} %get-tuple-element.8, f32[1536]{0:T(1024)S(1)} %select_reduce_fusion, s32[1536]{0:T(1024)S(1)} %dynamic_slice.16, s32[192]{0:T(256)S(1)} %select_reduce_fusion.5), kind=kOutput, calls=%fused_computation.13 | convolution fusion | flops 2417688320 | bytes 14170368 | tf_op jit(solution)/shard_map/qe,ke->qk/dot_general | solution.py:155
  176.4 1.7 collective-permute-start.1
  178.1 9.4 %fusion.6 = f32[192]{0:T(256)S(1)} fusion(bf16[192,4096]{1,0:T(8,128)(2,1)S(1)} %copy-done, bf16[1536,4096]{1,0:T(8,128)(2,1)} %all-gather.4.cloned.1.call-done, f32[1536]{0:T(1024)S(1)} %select_reduce_fusion, f32[192]{0:T(256)S(1)} %get-tuple-element.10, s32[192]{0:T(256)S(1)} %iota_add_fusion, s32[1536]{0:T(1024)S(1)} %dynamic_slice.16, ...), kind=kOutput, calls=%fused_computation.12 | convolution fusion | flops 2419457792 | bytes 14172672 | tf_op jit(solution)/shard_map/qe,ke->qk/dot_general | solution.py:155
  187.5 0.0 collective-permute-done.3
  187.5 0.0 collective-permute-done.1
  187.5 0.6 fusion.16
  (14 shorter events, 0.0 us)
Async XLA Ops:
  6.5 3.5 %copy-start.2 = (s32[6144]{0:T(1024)S(1)}, s32[6144]{0:T(1024)}, u32[]{:S(2)}) copy-start(s32[6144]{0:T(1024)} %param.5) | copy-start | bytes 73732
  6.5 28.5 %all-gather.6.cloned.1.call-start = ((), (), s32[]{:S(2)}) async-start(), calls=%async_computation.1 | async-start | bytes 1179648 | tf_op jit(solution)/shard_map/all_gather | solution.py:134
  7.4 28.9 %copy-start.1 = (bf16[192,4096]{1,0:T(8,128)(2,1)S(1)}, bf16[192,4096]{1,0:T(8,128)(2,1)}, u32[]{:S(2)}) copy-start(bf16[192,4096]{1,0:T(8,128)(2,1)} %param.4) | copy-start | bytes 4718596
  9.9 146.3 %all-gather.4.cloned.1.call-start = ((), (), s32[]{:S(2)}) async-start(), calls=%async_computation | async-start | bytes 14155776 | tf_op jit(solution)/shard_map/all_gather | solution.py:150
  39.8 1.4 copy-start
  39.8 3.9 %copy-start.3 = (s32[32,4]{0,1:T(4,128)S(1)}, s32[32,4]{0,1:T(4,128)}, u32[]{:S(2)}) copy-start(s32[32,4]{0,1:T(4,128)} %param.6) | copy-start | bytes 1540
  39.8 4.1 %copy-start.4 = (f32[32]{0:T(128)S(1)}, f32[32]{0:T(128)}, u32[]{:S(2)}) copy-start(f32[32]{0:T(128)} %param.7) | copy-start | bytes 388
  41.2 37.3 %collective-permute-start.2 = (bf16[192,4096]{1,0:T(8,128)(2,1)S(1)}, bf16[192,4096]{1,0:T(8,128)(2,1)S(1)}, u32[]{:S(2)}, u32[]{:S(2)}) collective-permute-start(bf16[192,4096]{1,0:T(8,128)(2,1)S(1)} %copy-done), channel_id=1, source_target_pairs={{8,0},{16,8},{24,16},{0,24},{9,1},{17,9},{25,17},{1,25},{10,2},{18... | collective-permute-start | bytes 4718600 | tf_op jit(solution)/shard_map/ppermute | solution.py:11
  43.9 122.9 %collective-permute-start = (bf16[192,4096]{1,0:T(8,128)(2,1)S(1)}, bf16[192,4096]{1,0:T(8,128)(2,1)}, u32[]{:S(2)}, u32[]{:S(2)}) collective-permute-start(bf16[192,4096]{1,0:T(8,128)(2,1)S(1)} %copy-done), channel_id=1, source_target_pairs={{24,0},{0,8},{8,16},{16,24},{25,1},{1,9},{9,17},{17,25},{26,2},{2,... | collective-permute-start | bytes 4718600 | tf_op jit(solution)/shard_map/ppermute | solution.py:11
  165.3 22.2 %collective-permute-start.3 = (f32[192]{0:T(256)S(1)}, f32[192]{0:T(256)S(1)}, u32[]{:S(2)}, u32[]{:S(2)}) collective-permute-start(f32[192]{0:T(256)S(1)} %fusion.8), channel_id=1, source_target_pairs={{24,0},{0,8},{8,16},{16,24},{25,1},{1,9},{9,17},{17,25},{26,2},{2,... | collective-permute-start | bytes 2312 | tf_op jit(solution)/shard_map/ppermute | solution.py:11
  176.4 11.1 %collective-permute-start.1 = (f32[192]{0:T(256)S(1)}, f32[192]{0:T(256)S(1)}, u32[]{:S(2)}, u32[]{:S(2)}) collective-permute-start(f32[192]{0:T(256)S(1)} %fusion.7), channel_id=1, source_target_pairs={{8,0},{16,8},{24,16},{0,24},{9,1},{17,9},{25,17},{1,25},{10,2},{18... | collective-permute-start | bytes 2312 | tf_op jit(solution)/shard_map/ppermute | solution.py:11
Sparse Core Ops, SparseCore 0:
  10.1 24.9 all-gather.5
  39.9 116.3 all-gather.3
